TPU v7x, 32 devices: a whole 2x2x4 slice. The times are simulated.
32 devices in a mesh: azi: 8 (over z, core), ax: 2 (over y), rad: 2 (over x).
Axes of the slice: x: 2, y: 2, z: 4, core: 2. Of those that a mesh axis runs over, the one named last changes fastest.
Arguments:
- fields: float32 [2, 512, 32, 1024], P(None, 'azi', 'ax', 'rad'), may hold values from 0 to 1.5
- swirl_speed: float32 [512, 32, 1024], P('azi', 'ax', 'rad'), may hold values from 0.05 to 0.35
- ghost_mask: int32 [512, 32, 1024], P('azi', 'ax', 'rad'), may hold values 0 or 1
- tile_flags: int32 [32, 32], P('azi', 'ax'), may hold values 0 or 1
- outlet_gain: float32 [2, 32], replicated, may hold values from 0.25 to 1
- feed_rate: float32 [8, 8, 8], P('azi'), may hold values from 0.05 to 0.5
- plenum: float32 [8, 8, 8, 1024], P('azi', None, None, 'rad'), may hold values from 0.5 to 1.5
- feed_target: int32 [8, 8, 8], P('azi'), may hold values from -1 to 255, as said below
Outputs:
- new_fields: float32 [2, 512, 32, 1024], P(None, 'azi', 'ax', 'rad')
Inputs may be any that keep to these rules, and one draw needn't show every extreme that they name: `feed_target`: entry i >= 0 names azimuthal cell i // 4 and axial cell i mod 4 of sector d; -1 marks an empty slot, and the used slots of a pair come first. At most 8 slots per pair are used; in every draw one sector receives 8 from every sector.
All inputs are finite; a program needn't handle non-finite values. No bound on the sum of `ghost_mask` or of `tile_flags` on one device may be relied on, other than what follows from the above.
Results may differ from a plain program's by a relative error of at most 0.00005.
Values sent between devices are 32-bit elements; how exact they have to be, the bound alone decides.
No kernel may reach another device: no remote copies, remote signals or barrier semaphores. Data moves between devices by JAX's collectives and lax.ppermute only.
A program may use at most 64 MiB of HBM per device.

v0:
```python
import math
import jax
import jax.numpy as jnp
from jax import lax
from jax.sharding import PartitionSpec as P

K = 32
TILE = 16
HEAD = 4


def with_halo(block, sides, width, periodic):
    for axis, dim in sides:
        count = lax.axis_size(axis)
        forward = [(i, i + 1) for i in range(count - 1)]
        if periodic:
            forward.append((count - 1, 0))
        backward = [(target, source) for source, target in forward]
        low = lax.ppermute(
            lax.slice_in_dim(block, block.shape[dim] - width, None, axis=dim), axis, forward
        )
        high = lax.ppermute(lax.slice_in_dim(block, 0, width, axis=dim), axis, backward)
        block = jnp.concatenate([low, block, high], axis=dim)
    return block


def phase_table(length, first_cell, cell_count, mode_count):
    theta_index = first_cell + jnp.arange(cell_count, dtype=jnp.int32)
    mode_order = jnp.arange(1, mode_count + 1, dtype=jnp.int32)
    phase_int = mode_order[:, None] * theta_index[None, :] % length
    angles = phase_int.astype(jnp.float32) * (2.0 * math.pi / length)
    return jnp.concatenate([jnp.cos(angles), jnp.sin(angles)], axis=0)


def body(fields, swirl_speed, ghost_mask, tile_flags, outlet_gain, feed_rate, plenum, feed_target):
    sectors = lax.axis_size("azi")
    sector = lax.axis_index("azi")
    slab_index = lax.axis_index("ax")
    slab_count = lax.axis_size("ax")
    sector_cells = fields.shape[1]
    depth_cells = fields.shape[2]
    radial_cells = fields.shape[3]
    length = sector_cells * sectors
    phase_rows = phase_table(length, sector * sector_cells, sector_cells, K)
    outlet_plane = fields[:, :, -1, :]
    partial_value = jnp.einsum(
        "mt,ctr->cmr", phase_rows, outlet_plane, precision=lax.Precision.HIGHEST
    )
    gain_both = jnp.concatenate([outlet_gain, outlet_gain], axis=1)
    mode_sums = lax.psum(partial_value, "azi")
    rebuilt = jnp.einsum(
        "mt,cmr->ctr",
        phase_rows,
        mode_sums * gain_both[:, :, None],
        precision=lax.Precision.HIGHEST,
    )
    ghost_plane = outlet_plane - rebuilt * (2.0 / math.sqrt(K * length))
    azimuth_pad = with_halo(fields, (("azi", 1),), 1, True)
    face_pad = with_halo(fields, (("ax", 2), ("rad", 3)), 1, False)
    theta_prev = azimuth_pad[:, :-2]
    theta_next = azimuth_pad[:, 2:]
    axial_prev = face_pad[:, :, :-2, 1:-1]
    axial_inner = face_pad[:, :, 2:, 1:-1]
    radial_prev = face_pad[:, :, 1:-1, :-2]
    radial_next = face_pad[:, :, 1:-1, 2:]
    is_outlet = slab_index == slab_count - 1
    top_layer = jnp.where(is_outlet, ghost_plane, axial_inner[:, :, -1, :])
    axial_next = jnp.concatenate([axial_inner[:, :, :-1, :], top_layer[:, :, None, :]], axis=2)
    laplace_term = (
        theta_prev + theta_next + axial_prev + axial_next + radial_prev + radial_next - 6.0 * fields
    )
    upwind_term = swirl_speed[None] * (fields - theta_prev)
    energy = fields[0]
    fuel_part = fields[1]
    tile_on = jnp.repeat(tile_flags, TILE, axis=0).astype(jnp.float32)
    inert = ghost_mask.astype(jnp.float32)
    reaction = (
        0.5 * tile_on[:, :, None] * (1.0 - inert) * fuel_part * jax.nn.sigmoid(4.0 * (energy - 0.5))
    )
    payload = feed_rate[0][:, :, None] * plenum[0]
    arrived = lax.all_to_all(payload, "azi", split_axis=0, concat_axis=0, tiled=True)
    targets = feed_target[0]
    occupied = targets >= 0
    row_index = jnp.where(
        occupied, targets // HEAD * depth_cells + targets % HEAD, sector_cells * depth_cells
    )
    feed_term = jnp.zeros((sector_cells * depth_cells, radial_cells), jnp.float32)
    feed_term = feed_term.at[row_index.reshape(-1)].add(
        arrived.reshape(-1, radial_cells), mode="drop"
    )
    feed_term = feed_term.reshape(sector_cells, depth_cells, radial_cells) * (
        slab_index == 0
    ).astype(jnp.float32)
    new_energy = energy - upwind_term[0] + 0.1 * laplace_term[0] + 2.0 * reaction
    new_fuel = fuel_part - upwind_term[1] + 0.1 * laplace_term[1] - reaction + feed_term
    return jnp.stack([new_energy, new_fuel], axis=0)


def solution(mesh):
    return jax.shard_map(
        body,
        mesh=mesh,
        in_specs=(
            P(None, "azi", "ax", "rad"),
            P("azi", "ax", "rad"),
            P("azi", "ax", "rad"),
            P("azi", "ax"),
            P(),
            P("azi", None, None),
            P("azi", None, None, "rad"),
            P("azi", None, None),
        ),
        out_specs=P(None, "azi", "ax", "rad"),
        check_vma=False,
    )
```

profile of v0, /device:TPU:0, one launch (start us, length us, event | category | flops | bytes accessed | tf_op | source)
XLA Modules:
  0.0 102.9 jit_solution(10300405495476792824)
XLA Ops:
  6.5 0.0 all-reduce.2.cloned.1.call-start
  6.5 2.8 %fusion.38 = (f32[2,64,1,512]{3,2,1,0:T(1,128)S(1)}, f32[2,64,1,512]{3,2,1,0:T(1,128)S(1)}) fusion(f32[2,64,16,512]{3,2,1,0:T(8,128)} %param.8), kind=kLoop, calls=%fused_computation.80 | loop fusion | bytes 1048576 | tf_op jit(solution)/shard_map/slice | solution.py:20
  9.3 0.2 fusion.31
  9.5 1.1 %convolution_bitcast_fusion = f32[2,64,512]{2,1,0:T(8,128)} fusion(f32[32,64]{1,0:T(8,128)S(1)} %get-tuple-element.14, f32[32,64]{1,0:T(8,128)S(1)} %get-tuple-element.13, f32[2,64,1,512]{3,2,1,0:T(1,128)S(1)} %get-tuple-element.11), kind=kOutput, calls=%fused_computation.41 | convolution fusion | flops 50335744 | bytes 540672 | tf_op jit(solution)/shard_map/mt,ctr->cmr/dot_general | solution.py:46
  10.6 0.0 all-reduce.2.cloned.1.call-update
  10.6 1.3 %collective-permute-start.3 = (f32[2,64,1,512]{3,1,0,2:T(8,128)S(1)}, f32[2,64,1,512]{3,1,0,2:T(8,128)S(1)}, u32[]{:S(2)}, u32[]{:S(2)}) collective-permute-start(f32[2,64,1,512]{3,1,0,2:T(8,128)S(1)} %copy.56), channel_id=1, source_target_pairs={{2,0},{3,1},{6,4},{7,5},{10,8},{11,9},{14,12},{15,13},{18,16},{19,... | collective-permute-start | bytes 786440 | tf_op jit(solution)/shard_map/ppermute | solution.py:22
  11.9 0.7 copy.55
  12.7 4.9 %collective-permute-start.2 = (f32[2,64,1,512]{3,1,0,2:T(8,128)}, f32[2,64,1,512]{3,1,0,2:T(8,128)S(1)}, u32[]{:S(2)}, u32[]{:S(2)}) collective-permute-start(f32[2,64,1,512]{3,1,0,2:T(8,128)} %copy.55), channel_id=1, source_target_pairs={{0,2},{1,3},{4,6},{5,7},{8,10},{9,11},{12,14},{13,15},{16,18},{17,... | collective-permute-start | bytes 786440 | tf_op jit(solution)/shard_map/ppermute | solution.py:19
  17.6 1.5 %fusion.37 = (f32[2,1,16,512]{3,2,1,0:T(8,128)S(1)}, f32[2,1,16,512]{3,2,1,0:T(8,128)}) fusion(f32[2,64,16,512]{3,2,1,0:T(8,128)} %param.8), kind=kLoop, calls=%fused_computation.79 | loop fusion | bytes 262144 | tf_op jit(solution)/shard_map/slice | solution.py:20
  19.1 0.0 collective-permute-start
  19.1 3.6 %collective-permute-start.1 = (f32[2,1,16,512]{3,2,1,0:T(8,128)}, f32[2,1,16,512]{3,2,1,0:T(8,128)}, u32[]{:S(2)}, u32[]{:S(2)}) collective-permute-start(f32[2,1,16,512]{3,2,1,0:T(8,128)} %get-tuple-element.10), channel_id=1, source_target_pairs={{4,0},{8,4},{12,8},{16,12},{20,16},{24,20},{28,24},{0,28},{5,1},{9... | collective-permute-start | bytes 196616 | tf_op jit(solution)/shard_map/ppermute | solution.py:22
  22.7 0.7 bitcast_multiply_fusion.2
  23.5 4.1 %all-to-all-start = ((f32[8,8,512]{2,1,0:T(8,128)}), f32[8,8,512]{2,1,0:T(8,128)S(1)}, u32[]{:S(2)}, u32[]{:S(2)}) async-start(f32[8,8,512]{2,1,0:T(8,128)} %bitcast_multiply_fusion.2), calls=%async_computation | async-start | bytes 262144 | tf_op jit(solution)/shard_map/all_to_all | solution.py:81
  27.6 0.0 copy-start.11
  27.6 0.0 copy-start.13
  27.6 0.0 copy-start.7
  27.6 5.2 %slice.74 = f32[2,64,15,512]{3,2,1,0:T(8,128)} slice(f32[2,64,16,512]{3,2,1,0:T(8,128)} %param.8), slice={[0:2], [0:64], [1:16], [0:512]} | slice | bytes 7864320 | tf_op jit(solution)/shard_map/slice | solution.py:68
  32.9 0.1 squeeze.26
  33.0 0.1 pad_maximum_fusion.13
  33.1 0.0 collective-permute-done
  33.1 6.9 %fusion.7 = f32[2,64,16,512]{3,2,1,0:T(8,128)} fusion(f32[2,64,16,512]{3,2,1,0:T(8,128)} %param.8, f32[2,1,16,512]{3,2,1,0:T(8,128)S(1)} %collective-permute-done, f32[64,16,512]{2,1,0:T(8,128)S(1)} %copy-done.7), kind=kLoop, calls=%fused_computation.17 | loop fusion | flops 3145728 | bytes 10551296 | tf_op jit(solution)/shard_map/mul | solution.py:72
  40.0 0.0 all-to-all-done
  40.0 1.5 %scatter_custom_fusion = f32[1024,512]{1,0:T(8,128)S(1)} fusion(s32[64]{0:T(128)S(1)} %fusion.33, f32[]{:T(128)} %constant.78.clone.1, f32[8,8,512]{2,1,0:T(8,128)S(1)} %all-to-all-done), kind=kCustom, calls=%fused_computation.43 | custom fusion | flops 32768 | bytes 2228228 | tf_op jit(solution)/shard_map/scatter-add | solution.py:88
  41.5 0.0 copy-start
  41.5 1.6 %broadcast_multiply_fusion = f32[1024,512]{1,0:T(8,128)} fusion(f32[1024,512]{1,0:T(8,128)S(1)} %scatter_custom_fusion, f32[]{:T(128)S(6)} %convert_element_type.21), kind=kLoop, calls=%fused_computation.42 | loop fusion | flops 524288 | bytes 4194308 | tf_op jit(solution)/shard_map/mul | solution.py:91
  43.1 0.0 collective-permute-done.2
  43.1 0.3 copy.43
  43.4 0.0 collective-permute-done.3
  43.4 0.7 copy-done.8
  44.1 0.3 copy.48
  44.4 0.3 copy-done
  44.7 1.0 pad_maximum_fusion.12
  45.7 0.5 copy.49
  46.1 3.7 %collective-permute-start.4 = (f32[2,64,18,1]{1,0,3,2:T(2,128)S(1)}, f32[2,64,18,1]{1,0,3,2:T(2,128)S(1)}, u32[]{:S(2)}, u32[]{:S(2)}) collective-permute-start(f32[2,64,18,1]{1,0,3,2:T(2,128)S(1)} %copy.49), channel_id=1, source_target_pairs={{0,1},{2,3},{4,5},{6,7},{8,9},{10,11},{12,13},{14,15},{16,17},{18,... | collective-permute-start | bytes 27656 | tf_op jit(solution)/shard_map/ppermute | solution.py:19
  49.9 0.5 copy.51
  50.3 1.5 %collective-permute-start.5 = (f32[2,64,18,1]{1,0,3,2:T(2,128)S(1)}, f32[2,64,18,1]{1,0,3,2:T(2,128)S(1)}, u32[]{:S(2)}, u32[]{:S(2)}) collective-permute-start(f32[2,64,18,1]{1,0,3,2:T(2,128)S(1)} %copy.51), channel_id=1, source_target_pairs={{1,0},{3,2},{5,4},{7,6},{9,8},{11,10},{13,12},{15,14},{17,16},{19,... | collective-permute-start | bytes 27656 | tf_op jit(solution)/shard_map/ppermute | solution.py:22
  51.8 17.9 %all-reduce.2.cloned.1.call-done = f32[2,64,512]{2,1,0:T(8,128)} async-done(((f32[2,64,512]{2,1,0:T(8,128)}), f32[2,64,512]{2,1,0:T(8,128)}) %all-reduce.2.cloned.1.call-update) | async-done | bytes 262160 | tf_op jit(solution)/shard_map/psum | solution.py:50
  69.7 1.5 %fusion.22 = f32[2,64,1,512]{3,1,0,2:T(8,128)S(1)} fusion(f32[2,64,1,512]{3,1,0,2:T(8,128)} %copy-done.8, f32[2,64,512]{2,1,0:T(8,128)} %all-reduce.2.cloned.1.call-done, f32[2,64]{1,0:T(2,128)S(1)} %pad_maximum_fusion.13, pred[]{:T(512)S(6)} %eq.10, f32[32,64]{1,0:T(8,128)S(1)} %get-tuple-element.14, f32[32,64]{1,0:T(8,128)S(1)} %get-tuple-element.13, ...), kind=kOutput, calls=%fused_computation.46 | convolution fusion | flops 50597888 | bytes 1065473 | tf_op jit(solution)/shard_map/mt,cmr->ctr/dot_general | solution.py:51
  71.2 1.0 copy.46
  72.1 0.0 collective-permute-done.4
  72.2 0.6 copy.50
  72.7 0.0 collective-permute-done.5
  72.8 1.7 %copy.52 = f32[2,64,18,1]{3,2,1,0:T(8,128)} copy(f32[2,64,18,1]{1,0,3,2:T(2,128)S(1)} %collective-permute-done.5) | data formatting | bytes 18432 | tf_op jit(solution)/shard_map/ppermute | solution.py:22
  74.4 0.0 collective-permute-done.1
  74.5 15.2 %fusion.1 = f32[2,64,16,512]{3,2,1,0:T(8,128)S(1)} fusion(f32[2,64,18,1]{3,2,1,0:T(8,128)} %copy.52, f32[2,64,1,512]{3,2,1,0:T(1,128)} %copy-done.6, f32[2,64,16,512]{3,2,1,0:T(8,128)} %param.8, f32[2,64,1,512]{3,2,1,0:T(1,128)S(1)} %copy-done.5, f32[2,64,18,1]{3,2,1,0:T(8,128)S(1)} %copy.50, f32[2,1,16,512]{3,2,1,0:T(8,128)} %collective-permute-done.1, ...), kind=kLoop, calls=%fused_computation.3 | loop fusion | flops 17825792 | bytes 13256704 | tf_op jit(solution)/shard_map/sub | solution.py:70
  89.7 2.5 %fusion.17 = (f32[1,64,16,512]{3,2,1,0:T(8,128)S(1)}, f32[64,16,512]{2,1,0:T(8,128)S(1)}) fusion(f32[2,64,16,512]{3,2,1,0:T(8,128)S(1)} %fusion.1, f32[2,64,16,512]{3,2,1,0:T(8,128)S(1)} %copy-done.2, f32[2,64,16,512]{3,2,1,0:T(8,128)S(1)} %copy-done.1, s32[64,16,512]{2,1,0:T(8,128)} %param.10, f32[64,16]{1,0:T(8,128)S(1)} %bitcast.71), kind=kLoop, calls=%fused_computation.31 | loop fusion | flops 7864320 | bytes 14684160 | tf_op jit(solution)/shard_map/stack | solution.py:96
  92.2 1.3 %fusion.12 = f32[1,64,16,512]{3,2,1,0:T(8,128)S(1)} fusion(f32[64,16,512]{2,1,0:T(8,128)S(1)} %bitcast.70, f32[64,16,512]{2,1,0:T(8,128)S(1)} %get-tuple-element.6, f32[2,64,16,512]{3,2,1,0:T(8,128)S(1)} %fusion.1, f32[2,64,16,512]{3,2,1,0:T(8,128)S(1)} %copy-done.2, f32[2,64,16,512]{3,2,1,0:T(8,128)S(1)} %copy-done.1), kind=kLoop, calls=%fused_computation.24 | loop fusion | flops 2621440 | bytes 12582912 | tf_op jit(solution)/shard_map/stack | solution.py:96
  93.6 2.5 %pad_maximum_fusion.9 = f32[2,64,16,512]{3,2,1,0:T(8,128)} fusion(f32[1,64,16,512]{3,2,1,0:T(8,128)S(1)} %fusion.12, f32[1,64,16,512]{3,2,1,0:T(8,128)S(1)} %get-tuple-element.5), kind=kLoop, calls=%fused_computation.18 | loop fusion | flops 1048576 | bytes 8388608 | tf_op jit(solution)/shard_map/stack | solution.py:96
  (28 shorter events, 0.1 us)
Async XLA Ops:
  6.5 16.2 %copy-start.10 = (f32[1,8,8]{2,1,0:T(8,128)S(1)}, f32[1,8,8]{2,1,0:T(8,128)}, u32[]{:S(2)}) copy-start(f32[1,8,8]{2,1,0:T(8,128)} %param.13) | copy-start | bytes 772
  6.5 16.2 %copy-start.9 = (f32[1,8,8,512]{3,2,1,0:T(8,128)S(1)}, f32[1,8,8,512]{3,2,1,0:T(8,128)}, u32[]{:S(2)}) copy-start(f32[1,8,8,512]{3,2,1,0:T(8,128)} %param.14) | copy-start | bytes 393220
  6.5 63.1 %all-reduce.2.cloned.1.call-start = ((), (), s32[]{:S(2)}) async-start(), calls=%async_computation.1 | async-start | bytes 524288 | tf_op jit(solution)/shard_map/psum | solution.py:50
  10.6 32.8 %collective-permute-start.3 = (f32[2,64,1,512]{3,1,0,2:T(8,128)S(1)}, f32[2,64,1,512]{3,1,0,2:T(8,128)S(1)}, u32[]{:S(2)}, u32[]{:S(2)}) collective-permute-start(f32[2,64,1,512]{3,1,0,2:T(8,128)S(1)} %copy.56), channel_id=1, source_target_pairs={{2,0},{3,1},{6,4},{7,5},{10,8},{11,9},{14,12},{15,13},{18,16},{19,... | collective-permute-start | bytes 786440 | tf_op jit(solution)/shard_map/ppermute | solution.py:22
  12.7 30.4 %collective-permute-start.2 = (f32[2,64,1,512]{3,1,0,2:T(8,128)}, f32[2,64,1,512]{3,1,0,2:T(8,128)S(1)}, u32[]{:S(2)}, u32[]{:S(2)}) collective-permute-start(f32[2,64,1,512]{3,1,0,2:T(8,128)} %copy.55), channel_id=1, source_target_pairs={{0,2},{1,3},{4,6},{5,7},{8,10},{9,11},{12,14},{13,15},{16,18},{17,... | collective-permute-start | bytes 786440 | tf_op jit(solution)/shard_map/ppermute | solution.py:19
  19.1 14.0 %collective-permute-start = (f32[2,1,16,512]{3,2,1,0:T(8,128)S(1)}, f32[2,1,16,512]{3,2,1,0:T(8,128)S(1)}, u32[]{:S(2)}, u32[]{:S(2)}) collective-permute-start(f32[2,1,16,512]{3,2,1,0:T(8,128)S(1)} %get-tuple-element.9), channel_id=1, source_target_pairs={{0,4},{4,8},{8,12},{12,16},{16,20},{20,24},{24,28},{28,0},{1,5},{5... | collective-permute-start | bytes 196616 | tf_op jit(solution)/shard_map/ppermute | solution.py:19
  19.1 55.3 %collective-permute-start.1 = (f32[2,1,16,512]{3,2,1,0:T(8,128)}, f32[2,1,16,512]{3,2,1,0:T(8,128)}, u32[]{:S(2)}, u32[]{:S(2)}) collective-permute-start(f32[2,1,16,512]{3,2,1,0:T(8,128)} %get-tuple-element.10), channel_id=1, source_target_pairs={{4,0},{8,4},{12,8},{16,12},{20,16},{24,20},{28,24},{0,28},{5,1},{9... | collective-permute-start | bytes 196616 | tf_op jit(solution)/shard_map/ppermute | solution.py:22
  23.5 16.6 %all-to-all-start = ((f32[8,8,512]{2,1,0:T(8,128)}), f32[8,8,512]{2,1,0:T(8,128)S(1)}, u32[]{:S(2)}, u32[]{:S(2)}) async-start(f32[8,8,512]{2,1,0:T(8,128)} %bitcast_multiply_fusion.2), calls=%async_computation | async-start | bytes 262144 | tf_op jit(solution)/shard_map/all_to_all | solution.py:81
  27.6 5.3 %copy-start.12 = (s32[4,16]{1,0:T(4,128)S(1)}, s32[4,16]{1,0:T(4,128)}, u32[]{:S(2)}) copy-start(s32[4,16]{1,0:T(4,128)} %param.11) | copy-start | bytes 772
  27.6 5.3 %copy-start.11 = (s32[1,8,8]{2,1,0:T(8,128)S(1)}, s32[1,8,8]{2,1,0:T(8,128)}, u32[]{:S(2)}) copy-start(s32[1,8,8]{2,1,0:T(8,128)} %param.15) | copy-start | bytes 772
  27.6 5.4 %copy-start.13 = (f32[2,32]{1,0:T(2,128)S(1)}, f32[2,32]{1,0:T(2,128)}, u32[]{:S(2)}) copy-start(f32[2,32]{1,0:T(2,128)} %param.12) | copy-start | bytes 772
  27.6 5.5 %copy-start.7 = (f32[64,16,512]{2,1,0:T(8,128)S(1)}, f32[64,16,512]{2,1,0:T(8,128)}, u32[]{:S(2)}) copy-start(f32[64,16,512]{2,1,0:T(8,128)} %param.9) | copy-start | bytes 6291460
  41.5 3.1 %copy-start = (f32[2,64,16,512]{3,2,1,0:T(8,128)S(1)}, f32[2,64,16,512]{3,2,1,0:T(8,128)}, u32[]{:S(2)}) copy-start(f32[2,64,16,512]{3,2,1,0:T(8,128)} %param.8) | copy-start | bytes 12582916
  43.4 2.3 %copy-start.4 = (f32[2,64,1,512]{3,2,1,0:T(1,128)}, f32[2,64,1,512]{3,2,1,0:T(1,128)S(1)}, u32[]{:S(2)}) copy-start(f32[2,64,1,512]{3,2,1,0:T(1,128)S(1)} %copy.43) | copy-start | bytes 786436
  43.4 0.7 copy-start.8
  44.7 1.0 copy-start.6
  46.1 26.0 %collective-permute-start.4 = (f32[2,64,18,1]{1,0,3,2:T(2,128)S(1)}, f32[2,64,18,1]{1,0,3,2:T(2,128)S(1)}, u32[]{:S(2)}, u32[]{:S(2)}) collective-permute-start(f32[2,64,18,1]{1,0,3,2:T(2,128)S(1)} %copy.49), channel_id=1, source_target_pairs={{0,1},{2,3},{4,5},{6,7},{8,9},{10,11},{12,13},{14,15},{16,17},{18,... | collective-permute-start | bytes 27656 | tf_op jit(solution)/shard_map/ppermute | solution.py:19
  50.3 22.4 %collective-permute-start.5 = (f32[2,64,18,1]{1,0,3,2:T(2,128)S(1)}, f32[2,64,18,1]{1,0,3,2:T(2,128)S(1)}, u32[]{:S(2)}, u32[]{:S(2)}) collective-permute-start(f32[2,64,18,1]{1,0,3,2:T(2,128)S(1)} %copy.51), channel_id=1, source_target_pairs={{1,0},{3,2},{5,4},{7,6},{9,8},{11,10},{13,12},{15,14},{17,16},{19,... | collective-permute-start | bytes 27656 | tf_op jit(solution)/shard_map/ppermute | solution.py:22
  71.2 3.3 %copy-start.5 = (f32[2,64,1,512]{3,2,1,0:T(1,128)S(1)}, f32[2,64,1,512]{3,2,1,0:T(1,128)}, u32[]{:S(2)}) copy-start(f32[2,64,1,512]{3,2,1,0:T(1,128)} %copy-done.4) | copy-start | bytes 786436
  74.4 15.2 %copy-start.2 = (f32[2,64,16,512]{3,2,1,0:T(8,128)S(1)}, f32[2,64,16,512]{3,2,1,0:T(8,128)}, u32[]{:S(2)}) copy-start(f32[2,64,16,512]{3,2,1,0:T(8,128)} %fusion.7) | copy-start | bytes 12582916
  74.4 15.2 %copy-start.1 = (f32[2,64,16,512]{3,2,1,0:T(8,128)S(1)}, f32[2,64,16,512]{3,2,1,0:T(8,128)}, u32[]{:S(2)}) copy-start(f32[2,64,16,512]{3,2,1,0:T(8,128)} %param.8) | copy-start | bytes 12582916
  89.7 2.5 %copy-start.3 = (f32[1024,512]{1,0:T(8,128)S(1)}, f32[1024,512]{1,0:T(8,128)}, u32[]{:S(2)}) copy-start(f32[1024,512]{1,0:T(8,128)} %broadcast_multiply_fusion) | copy-start | bytes 6291460
Sparse Core Ops, SparseCore 0:
  10.7 58.8 all-reduce.1
where the time goes:
time: 103 us
  other arithmetic  33.4 us (32%)
  starting transfers between devices  19.1 us (19%)
  waiting for transfers between devices  17.9 us (17%)
  local copies, waits for them, and re-layouts  16.1 us (16%)
  between operations  13.7 us (13%)
  matrix products  2.57 us (2%)
    psum x1, waiting for transfers between devices, body(): mode_sums = lax.psum(partial_value, 'azi')  17.9 us
    sub x1, other arithmetic, body(): theta_prev + theta_next + axial_prev + axial_next + radial_prev  15.2 us
    ppermute x3, starting transfers between devices, with_halo(): lax.ppermute(lax.slice_in_dim(block, block.shape[dim] - width, None, axis...  8.62 us
    mul x1, other arithmetic, body(): upwind_term = swirl_speed[None] * (fields - theta_prev)  6.95 us
    ppermute x3, starting transfers between devices, with_halo(): lax.ppermute(lax.slice_in_dim(block, 0, width, axis=dim), axis, backward)  6.36 us
    another operation x3, other arithmetic, body(): return jnp.stack([new_energy, new_fuel], axis=0)  6.28 us
    slice x1, local copies, waits for them, and re-layouts, body(): axial_inner[:, :, :-1, :]  5.25 us
    slice x3, local copies, waits for them, and re-layouts, with_halo(): lax.slice_in_dim(block, block.shape[dim] - width, None, axis=dim)  4.75 us
  transfers between devices with their start and end apart: 8, of which 1 were waited for; matrix products, arithmetic and copies ran while one was open for 25% of the time, Pallas kernels for 0%

commit v1 on v0

--- a/solution.py
+++ b/solution.py
@@ -47,7 +47,7 @@
         "mt,ctr->cmr", phase_rows, outlet_plane, precision=lax.Precision.HIGHEST
     )
     gain_both = jnp.concatenate([outlet_gain, outlet_gain], axis=1)
-    mode_sums = lax.psum(partial_value, "azi")
+    mode_sums = jnp.sum(lax.all_gather(partial_value, "azi"), axis=0)
     rebuilt = jnp.einsum(
         "mt,cmr->ctr",
         phase_rows,

time: 103 us -> 96.2 us (0.934)
  waiting for transfers between devices: 17.9 us -> 1.6 us
  other arithmetic: 33.4 us -> 39 us
  local copies, waits for them, and re-layouts: 16.1 us -> 19.5 us
  starting transfers between devices: 19.1 us -> 20.4 us
    psum x1 -> x0, waiting for transfers between devices: 17.9 us -> none  [body(): mode_sums = lax.psum(partial_value, 'azi')]
    slice x1, other arithmetic: 0.99 us -> 4.13 us  [with_halo(): lax.slice_in_dim(block, block.shape[dim] - width, None, axis=dim)]
    slice x1, local copies, waits for them, and re-layouts: 0.46 us -> 2.41 us  [with_halo(): lax.slice_in_dim(block, 0, width, axis=dim)]
    reduce_sum x0 -> x1, other arithmetic: none -> 1.82 us  [body(): mode_sums = jnp.sum(lax.all_gather(partial_value, 'azi'), axis=0)]
    unnamed x30 -> x28, local copies, waits for them, and re-layouts: 1.81 us -> 0.1 us
    ppermute x2, local copies, waits for them, and re-layouts: 0.85 us -> 2.52 us  [with_halo(): lax.ppermute(lax.slice_in_dim(block, block.shape[dim] - width, None, axis...]
    ppermute x3, waiting for transfers between devices: 0.01 us -> 1.58 us  [with_halo(): lax.ppermute(lax.slice_in_dim(block, 0, width, axis=dim), axis, backward)]
    slice x3, local copies, waits for them, and re-layouts: 4.75 us -> 6.1 us  [with_halo(): lax.slice_in_dim(block, block.shape[dim] - width, None, axis=dim)]
  transfers between devices with their start and end apart: 8 -> 8, of which waited for: 1 -> 1; matrix products, arithmetic and copies ran while one was open for 25% -> 35% of each run, Pallas kernels for 0% -> 0%
where the time goes in v1:
time: 96.2 us; the launch traced here: 95.6 us
  other arithmetic  39 us (41%)
  starting transfers between devices  20.4 us (21%)
  local copies, waits for them, and re-layouts  19.5 us (20%)
  between operations  13.7 us (14%)
  waiting for transfers between devices  1.6 us (2%)
  matrix products  1.55 us (2%)
    sub x1, other arithmetic, body(): theta_prev + theta_next + axial_prev + axial_next + radial_prev  15.7 us
    ppermute x3, starting transfers between devices, with_halo(): lax.ppermute(lax.slice_in_dim(block, block.shape[dim] - width, None, axis...  9.85 us
    mul x1, other arithmetic, body(): upwind_term = swirl_speed[None] * (fields - theta_prev)  6.98 us
    ppermute x3, starting transfers between devices, with_halo(): lax.ppermute(lax.slice_in_dim(block, 0, width, axis=dim), axis, backward)  6.35 us
    another operation x3, other arithmetic, body(): return jnp.stack([new_energy, new_fuel], axis=0)  6.28 us
    slice x3, local copies, waits for them, and re-layouts, with_halo(): lax.slice_in_dim(block, block.shape[dim] - width, None, axis=dim)  6.1 us
    slice x1, local copies, waits for them, and re-layouts, body(): axial_inner[:, :, :-1, :]  5.27 us
    all_to_all x1, starting transfers between devices, body(): lax.all_to_all(payload, 'azi', split_axis=0, concat_axis=0, tiled=True)  4.14 us
  transfers between devices with their start and end apart: 8, of which 1 were waited for; matrix products, arithmetic and copies ran while one was open for 35% of the time, Pallas kernels for 0%

profile of v1, /device:TPU:0, one launch (start us, length us, event | category | flops | bytes accessed | tf_op | source)
XLA Modules:
  0.0 95.6 jit_solution(17439996115639894036)
XLA Ops:
  6.5 0.0 all-gather.3.cloned.1.call-start
  6.5 2.8 %fusion.38 = (f32[2,64,1,512]{3,2,1,0:T(1,128)S(1)}, f32[2,64,1,512]{3,2,1,0:T(1,128)S(1)}) fusion(f32[2,64,16,512]{3,2,1,0:T(8,128)} %param.8), kind=kLoop, calls=%fused_computation.80 | loop fusion | bytes 1048576 | tf_op jit(solution)/shard_map/slice | solution.py:20
  9.3 0.2 fusion.31
  9.5 1.1 %convolution_bitcast_fusion = f32[2,64,512]{2,1,0:T(8,128)} fusion(f32[32,64]{1,0:T(8,128)S(1)} %get-tuple-element.14, f32[32,64]{1,0:T(8,128)S(1)} %get-tuple-element.13, f32[2,64,1,512]{3,2,1,0:T(1,128)S(1)} %get-tuple-element.11), kind=kOutput, calls=%fused_computation.41 | convolution fusion | flops 50335744 | bytes 540672 | tf_op jit(solution)/shard_map/mt,ctr->cmr/dot_general | solution.py:46
  10.6 0.0 all-gather.3.cloned.1.call-update
  10.6 1.3 %collective-permute-start.3 = (f32[2,64,1,512]{3,1,0,2:T(8,128)S(1)}, f32[2,64,1,512]{3,1,0,2:T(8,128)S(1)}, u32[]{:S(2)}, u32[]{:S(2)}) collective-permute-start(f32[2,64,1,512]{3,1,0,2:T(8,128)S(1)} %copy.58), channel_id=1, source_target_pairs={{2,0},{3,1},{6,4},{7,5},{10,8},{11,9},{14,12},{15,13},{18,16},{19,... | collective-permute-start | bytes 786440 | tf_op jit(solution)/shard_map/ppermute | solution.py:22
  12.0 5.6 %collective-permute-start.2 = (f32[2,64,1,512]{3,1,0,2:T(8,128)S(1)}, f32[2,64,1,512]{3,1,0,2:T(8,128)}, u32[]{:S(2)}, u32[]{:S(2)}) collective-permute-start(f32[2,64,1,512]{3,1,0,2:T(8,128)S(1)} %copy.57), channel_id=1, source_target_pairs={{0,2},{1,3},{4,6},{5,7},{8,10},{9,11},{12,14},{13,15},{16,18},{17,... | collective-permute-start | bytes 786440 | tf_op jit(solution)/shard_map/ppermute | solution.py:19
  17.6 1.5 %fusion.37 = (f32[2,1,16,512]{3,2,1,0:T(8,128)}, f32[2,1,16,512]{3,2,1,0:T(8,128)S(1)}) fusion(f32[2,64,16,512]{3,2,1,0:T(8,128)} %param.8), kind=kLoop, calls=%fused_computation.79 | loop fusion | bytes 262144 | tf_op jit(solution)/shard_map/slice | solution.py:20
  19.1 0.0 collective-permute-start
  19.1 3.6 %collective-permute-start.1 = (f32[2,1,16,512]{3,2,1,0:T(8,128)S(1)}, f32[2,1,16,512]{3,2,1,0:T(8,128)S(1)}, u32[]{:S(2)}, u32[]{:S(2)}) collective-permute-start(f32[2,1,16,512]{3,2,1,0:T(8,128)S(1)} %get-tuple-element.10), channel_id=1, source_target_pairs={{4,0},{8,4},{12,8},{16,12},{20,16},{24,20},{28,24},{0,28},{5,1},{9... | collective-permute-start | bytes 196616 | tf_op jit(solution)/shard_map/ppermute | solution.py:22
  22.7 0.7 bitcast_multiply_fusion.2
  23.4 4.1 %all-to-all-start = ((f32[8,8,512]{2,1,0:T(8,128)}), f32[8,8,512]{2,1,0:T(8,128)S(1)}, u32[]{:S(2)}, u32[]{:S(2)}) async-start(f32[8,8,512]{2,1,0:T(8,128)} %bitcast_multiply_fusion.2), calls=%async_computation | async-start | bytes 262144 | tf_op jit(solution)/shard_map/all_to_all | solution.py:81
  27.6 0.0 copy-start.11
  27.6 0.0 copy-start.12
  27.6 0.0 copy-start.5
  27.6 5.3 %slice.74 = f32[2,64,15,512]{3,2,1,0:T(8,128)} slice(f32[2,64,16,512]{3,2,1,0:T(8,128)} %param.8), slice={[0:2], [0:64], [1:16], [0:512]} | slice | bytes 7864320 | tf_op jit(solution)/shard_map/slice | solution.py:68
  32.9 0.1 squeeze.26
  33.0 0.0 copy-done.11
  33.0 0.0 copy-done.12
  33.0 0.1 pad_maximum_fusion.13
  33.1 0.0 collective-permute-done
  33.1 0.0 copy-done.5
  33.1 7.0 %fusion.7 = f32[2,64,16,512]{3,2,1,0:T(8,128)} fusion(f32[2,64,16,512]{3,2,1,0:T(8,128)} %param.8, f32[2,1,16,512]{3,2,1,0:T(8,128)S(1)} %collective-permute-done, f32[64,16,512]{2,1,0:T(8,128)S(1)} %copy-done.5), kind=kLoop, calls=%fused_computation.17 | loop fusion | flops 3145728 | bytes 10551296 | tf_op jit(solution)/shard_map/mul | solution.py:72
  40.1 0.0 all-to-all-done
  40.1 1.5 %scatter_custom_fusion = f32[1024,512]{1,0:T(8,128)S(1)} fusion(s32[64]{0:T(128)S(1)} %fusion.33, f32[]{:T(128)} %constant.71.clone.1, f32[8,8,512]{2,1,0:T(8,128)S(1)} %all-to-all-done), kind=kCustom, calls=%fused_computation.43 | custom fusion | flops 32768 | bytes 2228228 | tf_op jit(solution)/shard_map/scatter-add | solution.py:88
  41.5 0.0 collective-permute-done.2
  41.6 1.2 %copy.45 = f32[2,64,1,512]{3,2,1,0:T(1,128)S(1)} copy(f32[2,64,1,512]{3,1,0,2:T(8,128)} %collective-permute-done.2) | data formatting | bytes 524288 | tf_op jit(solution)/shard_map/ppermute | solution.py:19
  42.8 0.0 collective-permute-done.3
  42.8 0.3 copy.50
  43.1 4.1 %pad_maximum_fusion.12 = (f32[2,64,18,1]{3,2,1,0:T(8,128)}, f32[2,64,18,1]{3,2,1,0:T(8,128)}) fusion(f32[2,64,1,512]{3,2,1,0:T(1,128)S(1)} %copy.50, f32[2,64,16,512]{3,2,1,0:T(8,128)} %param.8, f32[2,64,1,512]{3,2,1,0:T(1,128)S(1)} %copy.45), kind=kLoop, calls=%fused_computation.37 | loop fusion | flops 9216 | bytes 4737024 | tf_op jit(solution)/shard_map/slice | solution.py:20
  47.2 1.8 %copy.51 = f32[2,64,18,1]{1,0,3,2:T(2,128)S(1)} copy(f32[2,64,18,1]{3,2,1,0:T(8,128)} %get-tuple-element.7) | data formatting | bytes 18432 | tf_op jit(solution)/shard_map/slice | solution.py:20
  49.1 4.2 %collective-permute-start.4 = (f32[2,64,18,1]{1,0,3,2:T(2,128)S(1)}, f32[2,64,18,1]{1,0,3,2:T(2,128)}, u32[]{:S(2)}, u32[]{:S(2)}) collective-permute-start(f32[2,64,18,1]{1,0,3,2:T(2,128)S(1)} %copy.51), channel_id=1, source_target_pairs={{0,1},{2,3},{4,5},{6,7},{8,9},{10,11},{12,13},{14,15},{16,17},{18,... | collective-permute-start | bytes 27656 | tf_op jit(solution)/shard_map/ppermute | solution.py:19
  53.3 2.4 %copy.53 = f32[2,64,18,1]{1,0,3,2:T(2,128)} copy(f32[2,64,18,1]{3,2,1,0:T(8,128)} %get-tuple-element.8) | data formatting | bytes 18432 | tf_op jit(solution)/shard_map/slice | solution.py:22
  55.7 1.5 %collective-permute-start.5 = (f32[2,64,18,1]{1,0,3,2:T(2,128)}, f32[2,64,18,1]{1,0,3,2:T(2,128)}, u32[]{:S(2)}, u32[]{:S(2)}) collective-permute-start(f32[2,64,18,1]{1,0,3,2:T(2,128)} %copy.53), channel_id=1, source_target_pairs={{1,0},{3,2},{5,4},{7,6},{9,8},{11,10},{13,12},{15,14},{17,16},{19,... | collective-permute-start | bytes 27656 | tf_op jit(solution)/shard_map/ppermute | solution.py:22
  57.2 1.6 %broadcast_multiply_fusion = f32[1024,512]{1,0:T(8,128)} fusion(f32[1024,512]{1,0:T(8,128)S(1)} %scatter_custom_fusion, f32[]{:T(128)S(6)} %convert_element_type.21), kind=kLoop, calls=%fused_computation.42 | loop fusion | flops 524288 | bytes 4194308 | tf_op jit(solution)/shard_map/mul | solution.py:91
  58.8 0.0 collective-permute-done.4
  58.8 1.3 %copy.52 = f32[2,64,18,1]{3,2,1,0:T(8,128)S(1)} copy(f32[2,64,18,1]{1,0,3,2:T(2,128)} %collective-permute-done.4) | data formatting | bytes 18432 | tf_op jit(solution)/shard_map/ppermute | solution.py:19
  60.1 1.6 %collective-permute-done.5 = f32[2,64,18,1]{1,0,3,2:T(2,128)} collective-permute-done((f32[2,64,18,1]{1,0,3,2:T(2,128)}, f32[2,64,18,1]{1,0,3,2:T(2,128)}, u32[]{:S(2)}, u32[]{:S(2)}) %collective-permute-start.5) | collective-permute-done | bytes 9248 | tf_op jit(solution)/shard_map/ppermute | solution.py:22
  61.7 2.5 %copy.54 = f32[2,64,18,1]{3,2,1,0:T(8,128)} copy(f32[2,64,18,1]{1,0,3,2:T(2,128)} %collective-permute-done.5) | data formatting | bytes 18432 | tf_op jit(solution)/shard_map/ppermute | solution.py:22
  64.1 1.8 %reduce_sum.9 = f32[2,64,512]{2,1,0:T(8,128)S(1)} reduce(f32[8,2,64,512]{3,2,1,0:T(8,128)} %bitcast.72, f32[]{:T(128)} %constant.71.clone.1), dimensions={0}, to_apply=%region_0.1 | reduce | flops 458752 | bytes 2359300 | tf_op jit(solution)/shard_map/reduce_sum | solution.py:50
  66.0 0.5 fusion.22
  66.4 0.3 copy.48
  66.7 0.0 collective-permute-done.1
  66.7 0.0 copy-start
  66.7 15.7 %fusion.1 = f32[2,64,16,512]{3,2,1,0:T(8,128)S(1)} fusion(f32[2,64,18,1]{3,2,1,0:T(8,128)} %copy.54, f32[2,64,1,512]{3,2,1,0:T(1,128)} %copy-done.4, f32[2,64,16,512]{3,2,1,0:T(8,128)} %param.8, f32[2,64,1,512]{3,2,1,0:T(1,128)} %copy-done.3, f32[2,64,18,1]{3,2,1,0:T(8,128)S(1)} %copy.52, f32[2,1,16,512]{3,2,1,0:T(8,128)S(1)} %collective-permute-done.1, ...), kind=kLoop, calls=%fused_computation.3 | loop fusion | flops 17825792 | bytes 13256704 | tf_op jit(solution)/shard_map/sub | solution.py:70
  82.5 2.5 %fusion.17 = (f32[1,64,16,512]{3,2,1,0:T(8,128)S(1)}, f32[64,16,512]{2,1,0:T(8,128)S(1)}) fusion(f32[2,64,16,512]{3,2,1,0:T(8,128)S(1)} %fusion.1, f32[2,64,16,512]{3,2,1,0:T(8,128)S(1)} %copy-done.1, f32[2,64,16,512]{3,2,1,0:T(8,128)S(1)} %copy-done, s32[64,16,512]{2,1,0:T(8,128)} %param.10, f32[64,16]{1,0:T(8,128)S(1)} %bitcast.73), kind=kLoop, calls=%fused_computation.31 | loop fusion | flops 7864320 | bytes 14684160 | tf_op jit(solution)/shard_map/stack | solution.py:96
  85.0 1.3 %fusion.12 = f32[1,64,16,512]{3,2,1,0:T(8,128)S(1)} fusion(f32[64,16,512]{2,1,0:T(8,128)S(1)} %bitcast.71, f32[64,16,512]{2,1,0:T(8,128)S(1)} %get-tuple-element.6, f32[2,64,16,512]{3,2,1,0:T(8,128)S(1)} %fusion.1, f32[2,64,16,512]{3,2,1,0:T(8,128)S(1)} %copy-done.1, f32[2,64,16,512]{3,2,1,0:T(8,128)S(1)} %copy-done), kind=kLoop, calls=%fused_computation.24 | loop fusion | flops 2621440 | bytes 12582912 | tf_op jit(solution)/shard_map/stack | solution.py:96
  86.3 2.5 %pad_maximum_fusion.9 = f32[2,64,16,512]{3,2,1,0:T(8,128)} fusion(f32[1,64,16,512]{3,2,1,0:T(8,128)S(1)} %fusion.12, f32[1,64,16,512]{3,2,1,0:T(8,128)S(1)} %get-tuple-element.5), kind=kLoop, calls=%fused_computation.18 | loop fusion | flops 1048576 | bytes 8388608 | tf_op jit(solution)/shard_map/stack | solution.py:96
  (27 shorter events, 0.1 us)
Async XLA Ops:
  6.5 16.1 %copy-start.9 = (f32[1,8,8]{2,1,0:T(8,128)S(1)}, f32[1,8,8]{2,1,0:T(8,128)}, u32[]{:S(2)}) copy-start(f32[1,8,8]{2,1,0:T(8,128)} %param.13) | copy-start | bytes 772
  6.5 16.1 %copy-start.8 = (f32[1,8,8,512]{3,2,1,0:T(8,128)S(1)}, f32[1,8,8,512]{3,2,1,0:T(8,128)}, u32[]{:S(2)}) copy-start(f32[1,8,8,512]{3,2,1,0:T(8,128)} %param.14) | copy-start | bytes 393220
  6.5 57.6 %all-gather.3.cloned.1.call-start = ((), (), s32[]{:S(2)}) async-start(), calls=%async_computation.1 | async-start | bytes 2359296 | tf_op jit(solution)/shard_map/all_gather | solution.py:50
  10.6 32.2 %collective-permute-start.3 = (f32[2,64,1,512]{3,1,0,2:T(8,128)S(1)}, f32[2,64,1,512]{3,1,0,2:T(8,128)S(1)}, u32[]{:S(2)}, u32[]{:S(2)}) collective-permute-start(f32[2,64,1,512]{3,1,0,2:T(8,128)S(1)} %copy.58), channel_id=1, source_target_pairs={{2,0},{3,1},{6,4},{7,5},{10,8},{11,9},{14,12},{15,13},{18,16},{19,... | collective-permute-start | bytes 786440 | tf_op jit(solution)/shard_map/ppermute | solution.py:22
  12.0 29.6 %collective-permute-start.2 = (f32[2,64,1,512]{3,1,0,2:T(8,128)S(1)}, f32[2,64,1,512]{3,1,0,2:T(8,128)}, u32[]{:S(2)}, u32[]{:S(2)}) collective-permute-start(f32[2,64,1,512]{3,1,0,2:T(8,128)S(1)} %copy.57), channel_id=1, source_target_pairs={{0,2},{1,3},{4,6},{5,7},{8,10},{9,11},{12,14},{13,15},{16,18},{17,... | collective-permute-start | bytes 786440 | tf_op jit(solution)/shard_map/ppermute | solution.py:19
  19.1 14.0 %collective-permute-start = (f32[2,1,16,512]{3,2,1,0:T(8,128)}, f32[2,1,16,512]{3,2,1,0:T(8,128)S(1)}, u32[]{:S(2)}, u32[]{:S(2)}) collective-permute-start(f32[2,1,16,512]{3,2,1,0:T(8,128)} %get-tuple-element.9), channel_id=1, source_target_pairs={{0,4},{4,8},{8,12},{12,16},{16,20},{20,24},{24,28},{28,0},{1,5},{5... | collective-permute-start | bytes 196616 | tf_op jit(solution)/shard_map/ppermute | solution.py:19
  19.1 47.7 %collective-permute-start.1 = (f32[2,1,16,512]{3,2,1,0:T(8,128)S(1)}, f32[2,1,16,512]{3,2,1,0:T(8,128)S(1)}, u32[]{:S(2)}, u32[]{:S(2)}) collective-permute-start(f32[2,1,16,512]{3,2,1,0:T(8,128)S(1)} %get-tuple-element.10), channel_id=1, source_target_pairs={{4,0},{8,4},{12,8},{16,12},{20,16},{24,20},{28,24},{0,28},{5,1},{9... | collective-permute-start | bytes 196616 | tf_op jit(solution)/shard_map/ppermute | solution.py:22
  23.4 16.7 %all-to-all-start = ((f32[8,8,512]{2,1,0:T(8,128)}), f32[8,8,512]{2,1,0:T(8,128)S(1)}, u32[]{:S(2)}, u32[]{:S(2)}) async-start(f32[8,8,512]{2,1,0:T(8,128)} %bitcast_multiply_fusion.2), calls=%async_computation | async-start | bytes 262144 | tf_op jit(solution)/shard_map/all_to_all | solution.py:81
  27.6 5.3 %copy-start.10 = (s32[1,8,8]{2,1,0:T(8,128)S(1)}, s32[1,8,8]{2,1,0:T(8,128)}, u32[]{:S(2)}) copy-start(s32[1,8,8]{2,1,0:T(8,128)} %param.15) | copy-start | bytes 772
  27.6 5.4 %copy-start.11 = (s32[4,16]{1,0:T(4,128)S(1)}, s32[4,16]{1,0:T(4,128)}, u32[]{:S(2)}) copy-start(s32[4,16]{1,0:T(4,128)} %param.11) | copy-start | bytes 772
  27.6 5.4 %copy-start.12 = (f32[2,32]{1,0:T(2,128)S(1)}, f32[2,32]{1,0:T(2,128)}, u32[]{:S(2)}) copy-start(f32[2,32]{1,0:T(2,128)} %param.12) | copy-start | bytes 772
  27.6 5.5 %copy-start.5 = (f32[64,16,512]{2,1,0:T(8,128)S(1)}, f32[64,16,512]{2,1,0:T(8,128)}, u32[]{:S(2)}) copy-start(f32[64,16,512]{2,1,0:T(8,128)} %param.9) | copy-start | bytes 6291460
  42.8 4.5 %copy-start.3 = (f32[2,64,1,512]{3,2,1,0:T(1,128)}, f32[2,64,1,512]{3,2,1,0:T(1,128)S(1)}, u32[]{:S(2)}) copy-start(f32[2,64,1,512]{3,2,1,0:T(1,128)S(1)} %copy.45) | copy-start | bytes 786436
  42.8 4.4 %copy-start.6 = (f32[2,64,1,512]{3,1,0,2:T(8,128)}, f32[2,64,1,512]{3,1,0,2:T(8,128)S(1)}, u32[]{:S(2)}) copy-start(f32[2,64,1,512]{3,1,0,2:T(8,128)S(1)} %collective-permute-done.3) | copy-start | bytes 786436
  43.1 4.1 %copy-start.4 = (f32[2,64,1,512]{3,2,1,0:T(1,128)}, f32[2,64,1,512]{3,2,1,0:T(1,128)S(1)}, u32[]{:S(2)}) copy-start(f32[2,64,1,512]{3,2,1,0:T(1,128)S(1)} %copy.50) | copy-start | bytes 786436
  49.1 9.7 %collective-permute-start.4 = (f32[2,64,18,1]{1,0,3,2:T(2,128)S(1)}, f32[2,64,18,1]{1,0,3,2:T(2,128)}, u32[]{:S(2)}, u32[]{:S(2)}) collective-permute-start(f32[2,64,18,1]{1,0,3,2:T(2,128)S(1)} %copy.51), channel_id=1, source_target_pairs={{0,1},{2,3},{4,5},{6,7},{8,9},{10,11},{12,13},{14,15},{16,17},{18,... | collective-permute-start | bytes 27656 | tf_op jit(solution)/shard_map/ppermute | solution.py:19
  55.7 6.0 %collective-permute-start.5 = (f32[2,64,18,1]{1,0,3,2:T(2,128)}, f32[2,64,18,1]{1,0,3,2:T(2,128)}, u32[]{:S(2)}, u32[]{:S(2)}) collective-permute-start(f32[2,64,18,1]{1,0,3,2:T(2,128)} %copy.53), channel_id=1, source_target_pairs={{1,0},{3,2},{5,4},{7,6},{9,8},{11,10},{13,12},{15,14},{17,16},{19,... | collective-permute-start | bytes 27656 | tf_op jit(solution)/shard_map/ppermute | solution.py:22
  60.1 5.9 %copy-start.7 = (f32[2,64,1,512]{3,1,0,2:T(8,128)S(1)}, f32[2,64,1,512]{3,1,0,2:T(8,128)}, u32[]{:S(2)}) copy-start(f32[2,64,1,512]{3,1,0,2:T(8,128)} %copy-done.6) | copy-start | bytes 786436
  66.7 15.8 %copy-start.1 = (f32[2,64,16,512]{3,2,1,0:T(8,128)S(1)}, f32[2,64,16,512]{3,2,1,0:T(8,128)}, u32[]{:S(2)}) copy-start(f32[2,64,16,512]{3,2,1,0:T(8,128)} %fusion.7) | copy-start | bytes 12582916
  66.7 15.7 %copy-start = (f32[2,64,16,512]{3,2,1,0:T(8,128)S(1)}, f32[2,64,16,512]{3,2,1,0:T(8,128)}, u32[]{:S(2)}) copy-start(f32[2,64,16,512]{3,2,1,0:T(8,128)} %param.8) | copy-start | bytes 12582916
  82.5 2.5 %copy-start.2 = (f32[1024,512]{1,0:T(8,128)S(1)}, f32[1024,512]{1,0:T(8,128)}, u32[]{:S(2)}) copy-start(f32[1024,512]{1,0:T(8,128)} %broadcast_multiply_fusion) | copy-start | bytes 6291460
Sparse Core Ops, SparseCore 0:
  10.7 35.9 all-gather.2
